TPU v7x, 32 devices: a whole 2x2x4 slice. The times are simulated.
32 devices in a mesh: owner: 4 (over z), rows: 8 (over y, x, core).
Axes of the slice: x: 2, y: 2, z: 4, core: 2. Of those that a mesh axis runs over, the one named last changes fastest.
Arguments:
- w_gate: float32 [128, 2048, 768], P('owner', 'rows'), may hold values from -0.1875 to 0.1875
- w_up: float32 [128, 2048, 768], P('owner', 'rows'), may hold values from -0.1875 to 0.1875
- router_weight: float32 [2048, 128], P('rows', 'owner'), may hold values from -0.125 to 0.125
- router_gain: float32 [2048], P('rows'), may hold values from 0.25 to 1.75
Outputs:
- serve_gate: bfloat16 [128, 2048, 768], P('owner', None, 'rows')
- serve_up: bfloat16 [128, 2048, 768], P('owner', None, 'rows')
- scale_gate: float32 [128, 768], P('owner', 'rows')
- scale_up: float32 [128, 768], P('owner', 'rows')
- serve_router: bfloat16 [2048, 128], replicated
All inputs are finite; a program needn't handle non-finite values. Where the computation divides by a largest or mean magnitude, that divisor is 1e-20 or more.
Results may differ from a plain program's by a relative error of at most 0.001.
Values may be sent and summed in bfloat16 or wider, within the bound.
No kernel may reach another device: no remote copies, remote signals or barrier semaphores. Data moves between devices by JAX's collectives and lax.ppermute only.
A program may use at most 192 MiB of HBM per device.

v0:
```python
import jax
import jax.numpy as jnp
from jax import lax
from jax.sharding import PartitionSpec as P

D_MODEL = 2048


def on_device(w_gate, w_up, router_weight, router_gain):
    total_gate, total_up = lax.psum(
        (jnp.sum(jnp.abs(w_gate), axis=1), jnp.sum(jnp.abs(w_up), axis=1)), "rows"
    )
    scale_gate = total_gate / D_MODEL
    scale_up = total_up / D_MODEL
    narrow_gate, narrow_up = (
        (w_gate / jnp.expand_dims(scale_gate, 1)).astype(jnp.bfloat16),
        (w_up / jnp.expand_dims(scale_up, 1)).astype(jnp.bfloat16),
    )
    serve_gate, serve_up = (
        lax.all_to_all(narrow_gate, "rows", split_axis=2, concat_axis=1, tiled=True),
        lax.all_to_all(narrow_up, "rows", split_axis=2, concat_axis=1, tiled=True),
    )
    scale_gate = lax.dynamic_slice_in_dim(
        scale_gate, lax.axis_index("rows") * serve_gate.shape[2], serve_gate.shape[2], axis=1
    )
    scale_up = lax.dynamic_slice_in_dim(
        scale_up, lax.axis_index("rows") * serve_up.shape[2], serve_up.shape[2], axis=1
    )
    part_router = (router_weight * router_gain[:, None]).astype(jnp.bfloat16)
    row_router = lax.all_gather(part_router, "rows", axis=0, tiled=True)
    serve_router = lax.all_gather(row_router, "owner", axis=1, tiled=True)
    return (serve_gate, serve_up, scale_gate, scale_up, serve_router)


def solution(mesh):
    placed = (P("owner", "rows", None), P("owner", "rows", None), P("rows", "owner"), P("rows"))
    return jax.shard_map(
        on_device,
        mesh=mesh,
        in_specs=placed,
        out_specs=(
            P("owner", None, "rows"),
            P("owner", None, "rows"),
            P("owner", "rows"),
            P("owner", "rows"),
            P(),
        ),
        check_vma=False,
    )
```

profile of v0, /device:TPU:0, one launch (start us, length us, event | category | flops | bytes accessed | tf_op | source)
XLA Modules:
  0.0 481.1 jit_solution(11326135817132377053)
XLA Ops:
  7.2 0.0 all-reduce.3.cloned.1.call-start
  7.2 17.4 %abs_reduce_fusion = (f32[32,768]{1,0:T(8,128)}, f32[32,768]{1,0:T(8,128)}) fusion(f32[32,256,768]{2,1,0:T(8,128)} %param.5, f32[32,256,768]{2,1,0:T(8,128)} %param.4), kind=kLoop, calls=%fused_computation.1 | loop fusion | flops 25116672 | bytes 50528256 | tf_op jit(solution)/shard_map/reduce_sum | solution.py:11
  24.6 0.0 all-reduce.3.cloned.1.call-update
  24.7 25.1 %copy.25 = f32[32,256,768]{1,0,2:T(8,128)} copy(f32[32,256,768]{2,1,0:T(8,128)} %param.5) | data formatting | bytes 50331648 | tf_op args[1]
  49.8 31.5 %all-reduce.3.cloned.1.call-done = (f32[32,768]{1,0:T(8,128)}, f32[32,768]{1,0:T(8,128)}) async-done(((f32[32,768]{1,0:T(8,128)}, f32[32,768]{1,0:T(8,128)}), (f32[32,768]{1,0:T(8,128)}, f32[32,768]{1,0:T(8,128)})) %all-reduce.3.cloned.1.call-update) | async-done | bytes 196624 | tf_op jit(solution)/shard_map/psum | solution.py:10
  81.3 0.9 broadcast_multiply_fusion
  82.2 0.2 copy.24
  82.4 14.1 %divide_convert_fusion = bf16[32,256,768]{1,0,2:T(8,128)(2,1)} fusion(f32[32,256,768]{1,0,2:T(8,128)} %copy.25, f32[32,768]{0,1:T(8,128)S(1)} %copy.24), kind=kLoop, calls=%fused_computation | loop fusion | flops 12582912 | bytes 37847040 | tf_op jit(solution)/shard_map/convert_element_type | solution.py:17
  96.5 5.4 %all-to-all-start.1 = ((bf16[32,256,768]{1,0,2:T(8,128)(2,1)}), bf16[32,256,768]{1,0,2:T(8,128)(2,1)}, u32[]{:S(2)}, u32[]{:S(2)}) async-start(bf16[32,256,768]{1,0,2:T(8,128)(2,1)} %divide_convert_fusion), calls=%async_computation.1 | async-start | bytes 25165824 | tf_op jit(solution)/shard_map/all_to_all | solution.py:21
  101.9 25.1 %copy.21 = f32[32,256,768]{1,0,2:T(8,128)} copy(f32[32,256,768]{2,1,0:T(8,128)} %param.4) | data formatting | bytes 50331648 | tf_op args[0]
  127.1 0.2 copy.20
  127.2 0.0 copy-start.1
  127.3 14.1 %divide_convert_fusion.1 = bf16[32,256,768]{1,0,2:T(8,128)(2,1)} fusion(f32[32,256,768]{1,0,2:T(8,128)} %copy.21, f32[32,768]{0,1:T(8,128)S(1)} %copy.20), kind=kLoop, calls=%fused_computation.2 | loop fusion | flops 12582912 | bytes 37847040 | tf_op jit(solution)/shard_map/convert_element_type | solution.py:16
  141.4 99.5 %all-to-all-done.1 = bf16[32,256,768]{1,0,2:T(8,128)(2,1)} async-done(((bf16[32,256,768]{1,0,2:T(8,128)(2,1)}), bf16[32,256,768]{1,0,2:T(8,128)(2,1)}, u32[]{:S(2)}, u32[]{:S(2)}) %all-to-all-start.1) | async-done | bytes 12582944 | tf_op jit(solution)/shard_map/all_to_all | solution.py:21
  240.9 5.4 %all-to-all-start = ((bf16[32,256,768]{1,0,2:T(8,128)(2,1)}), bf16[32,256,768]{1,0,2:T(8,128)(2,1)}, u32[]{:S(2)}, u32[]{:S(2)}) async-start(bf16[32,256,768]{1,0,2:T(8,128)(2,1)} %divide_convert_fusion.1), calls=%async_computation | async-start | bytes 25165824 | tf_op jit(solution)/shard_map/all_to_all | solution.py:20
  246.3 142.4 %all_gather.6 = bf16[2048,32]{0,1:T(8,128)(2,1)S(1)} all-gather(bf16[256,32]{0,1:T(8,128)(2,1)S(1)} %multiply_convert_fusion), channel_id=1, replica_groups=mesh['owner'=4,'rows'=8] {'rows'}, dimensions={0}, use_global_device_ids=true | all-gather | bytes 147456 | tf_op jit(solution)/shard_map/all_gather | solution.py:30
  388.8 16.1 %all_gather.7 = bf16[2048,128]{0,1:T(8,128)(2,1)S(1)} all-gather(bf16[2048,32]{0,1:T(8,128)(2,1)S(1)} %all_gather.6), channel_id=1, replica_groups=mesh['owner'=4,'rows'=8] {'owner'}, dimensions={1}, use_global_device_ids=true | all-gather | bytes 655360 | tf_op jit(solution)/shard_map/all_gather | solution.py:31
  404.8 1.0 copy.28
  405.8 0.7 constant_dynamic-slice_fusion
  406.5 0.7 constant_dynamic-slice_fusion.1
  407.2 14.1 %copy.27 = bf16[32,8,256,96]{2,1,3,0:T(8,128)(2,1)} copy(bf16[32,8,256,96]{2,0,3,1:T(8,128)(2,1)} %bitcast.5) | data formatting | bytes 25165824 | tf_op jit(solution)/shard_map/all_to_all | solution.py:21
  421.2 19.5 %all_to_all.33 = bf16[32,2048,96]{1,2,0:T(8,128)(2,1)} reshape(bf16[32,8,256,96]{2,1,3,0:T(8,128)(2,1)} %copy.27) | data formatting | bytes 25165824 | tf_op jit(solution)/shard_map/all_to_all | solution.py:21
  440.7 14.1 %copy.23 = bf16[32,8,256,96]{2,1,3,0:T(8,128)(2,1)} copy(bf16[32,8,256,96]{2,0,3,1:T(8,128)(2,1)} %bitcast.2) | data formatting | bytes 25165824 | tf_op jit(solution)/shard_map/all_to_all | solution.py:20
  454.8 19.5 %all_to_all.29 = bf16[32,2048,96]{1,2,0:T(8,128)(2,1)} reshape(bf16[32,8,256,96]{2,1,3,0:T(8,128)(2,1)} %copy.23) | data formatting | bytes 25165824 | tf_op jit(solution)/shard_map/all_to_all | solution.py:20
  (8 shorter events, 0.0 us)
Async XLA Ops:
  7.2 74.2 %all-reduce.3.cloned.1.call-start = ((), (), s32[]{:S(2)}) async-start(), calls=%async_computation.2 | async-start | bytes 393216 | tf_op jit(solution)/shard_map/psum | solution.py:10
  96.5 144.4 %all-to-all-start.1 = ((bf16[32,256,768]{1,0,2:T(8,128)(2,1)}), bf16[32,256,768]{1,0,2:T(8,128)(2,1)}, u32[]{:S(2)}, u32[]{:S(2)}) async-start(bf16[32,256,768]{1,0,2:T(8,128)(2,1)} %divide_convert_fusion), calls=%async_computation.1 | async-start | bytes 25165824 | tf_op jit(solution)/shard_map/all_to_all | solution.py:21
  101.9 25.1 %copy-start = (f32[32,768]{1,0:T(8,128)S(1)}, f32[32,768]{1,0:T(8,128)}, u32[]{:S(2)}) copy-start(f32[32,768]{1,0:T(8,128)} %get-tuple-element.10) | copy-start | bytes 294916
  127.2 119.0 %copy-start.1 = (f32[256,32]{0,1:T(8,128)S(1)}, f32[256,32]{0,1:T(8,128)}, u32[]{:S(2)}) copy-start(f32[256,32]{0,1:T(8,128)} %param.6) | copy-start | bytes 98308
  127.3 119.0 %copy-start.2 = (f32[256]{0:T(256)S(1)}, f32[256]{0:T(256)}, u32[]{:S(2)}) copy-start(f32[256]{0:T(256)} %param.7) | copy-start | bytes 3076
  240.9 199.8 %all-to-all-start = ((bf16[32,256,768]{1,0,2:T(8,128)(2,1)}), bf16[32,256,768]{1,0,2:T(8,128)(2,1)}, u32[]{:S(2)}, u32[]{:S(2)}) async-start(bf16[32,256,768]{1,0,2:T(8,128)(2,1)} %divide_convert_fusion.1), calls=%async_computation | async-start | bytes 25165824 | tf_op jit(solution)/shard_map/all_to_all | solution.py:20
Sparse Core Ops, SparseCore 0:
  24.8 56.4 all-reduce.2
where the time goes:
time: 483 us; the launch traced here: 481 us
  blocking collectives  158 us (33%)
  waiting for transfers between devices  131 us (27%)
  local copies, waits for them, and re-layouts  120 us (25%)
  other arithmetic  46.6 us (10%)
  between operations  14.1 us (3%)
  starting transfers between devices  10.8 us (2%)
    all_gather x1, blocking collectives, on_device(): row_router = lax.all_gather(part_router, 'rows', axis=0, tiled=True)  142 us
    all_to_all x1, waiting for transfers between devices, on_device(): lax.all_to_all(narrow_up, 'rows', split_axis=2, concat_axis=1, tiled=True)  99.5 us
    unnamed x9, local copies, waits for them, and re-layouts  51.3 us
    all_to_all x2, local copies, waits for them, and re-layouts, on_device(): lax.all_to_all(narrow_gate, 'rows', split_axis=2, concat_axis=1, tiled=True)  33.6 us
    all_to_all x2, local copies, waits for them, and re-layouts, on_device(): lax.all_to_all(narrow_up, 'rows', split_axis=2, concat_axis=1, tiled=True)  33.6 us
    psum x1, waiting for transfers between devices, on_device(): lax.psum((jnp.sum(jnp.abs(w_gate), axis=1), jnp.sum(jnp.abs(w_up), axis=1...  31.5 us
    reduce_sum x1, other arithmetic, on_device(): jnp.sum(jnp.abs(w_up), axis=1)  17.4 us
    all_gather x1, blocking collectives, on_device(): serve_router = lax.all_gather(row_router, 'owner', axis=1, tiled=True)  16.1 us
  transfers between devices with their start and end apart: 3, of which 2 were waited for; matrix products, arithmetic and copies ran while one was open for 17% of the time, Pallas kernels for 0%

commit v1 on v0

--- a/solution.py
+++ b/solution.py
@@ -27,7 +27,12 @@
         scale_up, lax.axis_index("rows") * serve_up.shape[2], serve_up.shape[2], axis=1
     )
     part_router = (router_weight * router_gain[:, None]).astype(jnp.bfloat16)
-    row_router = lax.all_gather(part_router, "rows", axis=0, tiled=True)
+    ring = [part_router]
+    for hop in range(7):
+        ring.append(lax.ppermute(ring[-1], "rows", [(dev, (dev + 1) % 8) for dev in range(8)]))
+    row_router = jnp.roll(
+        jnp.concatenate(ring[::-1], axis=0), (lax.axis_index("rows") + 1) * ring[0].shape[0], axis=0
+    )
     serve_router = lax.all_gather(row_router, "owner", axis=1, tiled=True)
     return (serve_gate, serve_up, scale_gate, scale_up, serve_router)
 

time: 483 us -> 503 us (1.041)
  waiting for transfers between devices: 131 us -> 292 us
  blocking collectives: 158 us -> 16.2 us
    ppermute x0 -> x7, waiting for transfers between devices: none -> 161 us  [on_device(): lax.ppermute(ring[-1], 'rows', [(dev, (dev + 1) % 8) for dev in range(8)])]
    all_gather x1 -> x0, blocking collectives: 142 us -> none  [on_device(): row_router = lax.all_gather(part_router, 'rows', axis=0, tiled=True)]
    all_to_all x1, waiting for transfers between devices: 0.01 us -> 99.6 us  [on_device(): lax.all_to_all(narrow_gate, 'rows', split_axis=2, concat_axis=1, tiled=True)]
    all_to_all x1, waiting for transfers between devices: 99.5 us -> 0.01 us  [on_device(): lax.all_to_all(narrow_up, 'rows', split_axis=2, concat_axis=1, tiled=True)]
    unnamed x9 -> x23, local copies, waits for them, and re-layouts: 51.3 us -> 51.2 us
  transfers between devices with their start and end apart: 3 -> 10, of which waited for: 2 -> 9; matrix products, arithmetic and copies ran while one was open for 17% -> 16% of each run, Pallas kernels for 0% -> 0%
where the time goes in v1:
time: 503 us; the launch traced here: 501 us
  waiting for transfers between devices  292 us (58%)
  local copies, waits for them, and re-layouts  120 us (24%)
  other arithmetic  46.6 us (9%)
  blocking collectives  16.2 us (3%)
  between operations  14.2 us (3%)
  starting transfers between devices  11.2 us (2%)
    ppermute x7, waiting for transfers between devices, on_device(): lax.ppermute(ring[-1], 'rows', [(dev, (dev + 1) % 8) for dev in range(8)])  161 us
    all_to_all x1, waiting for transfers between devices, on_device(): lax.all_to_all(narrow_gate, 'rows', split_axis=2, concat_axis=1, tiled=True)  99.6 us
    unnamed x23, local copies, waits for them, and re-layouts  51.2 us
    all_to_all x2, local copies, waits for them, and re-layouts, on_device(): lax.all_to_all(narrow_gate, 'rows', split_axis=2, concat_axis=1, tiled=True)  33.5 us
    all_to_all x2, local copies, waits for them, and re-layouts, on_device(): lax.all_to_all(narrow_up, 'rows', split_axis=2, concat_axis=1, tiled=True)  33.5 us
    psum x1, waiting for transfers between devices, on_device(): lax.psum((jnp.sum(jnp.abs(w_gate), axis=1), jnp.sum(jnp.abs(w_up), axis=1...  31.6 us
    reduce_sum x1, other arithmetic, on_device(): jnp.sum(jnp.abs(w_up), axis=1)  17.4 us
    all_gather x1, blocking collectives, on_device(): serve_router = lax.all_gather(row_router, 'owner', axis=1, tiled=True)  16.2 us
  transfers between devices with their start and end apart: 10, of which 9 were waited for; matrix products, arithmetic and copies ran while one was open for 16% of the time, Pallas kernels for 0%

profile of v1, /device:TPU:0, one launch (start us, length us, event | category | flops | bytes accessed | tf_op | source)
XLA Modules:
  0.0 500.6 jit_solution(17368511541042503295)
XLA Ops:
  7.2 17.4 %abs_reduce_fusion = (f32[32,768]{1,0:T(8,128)}, f32[32,768]{1,0:T(8,128)}) fusion(f32[32,256,768]{2,1,0:T(8,128)} %param.5, f32[32,256,768]{2,1,0:T(8,128)} %param.4), kind=kLoop, calls=%fused_computation.1 | loop fusion | flops 25116672 | bytes 50528256 | tf_op jit(solution)/shard_map/reduce_sum | solution.py:11
  24.7 25.0 %copy.21 = f32[32,256,768]{1,0,2:T(8,128)} copy(f32[32,256,768]{2,1,0:T(8,128)} %param.4) | data formatting | bytes 50331648 | tf_op args[0]
  49.7 31.6 %all-reduce.3.cloned.1.call-done = (f32[32,768]{1,0:T(8,128)}, f32[32,768]{1,0:T(8,128)}) async-done(((f32[32,768]{1,0:T(8,128)}, f32[32,768]{1,0:T(8,128)}), (f32[32,768]{1,0:T(8,128)}, f32[32,768]{1,0:T(8,128)})) %all-reduce.3.cloned.1.call-update) | async-done | bytes 196624 | tf_op jit(solution)/shard_map/psum | solution.py:10
  81.3 0.9 broadcast_multiply_fusion.1
  82.4 14.1 %divide_convert_fusion.1 = bf16[32,256,768]{1,0,2:T(8,128)(2,1)} fusion(f32[32,256,768]{1,0,2:T(8,128)} %copy.21, f32[32,768]{0,1:T(8,128)S(1)} %copy.20), kind=kLoop, calls=%fused_computation.2 | loop fusion | flops 12582912 | bytes 37847040 | tf_op jit(solution)/shard_map/convert_element_type | solution.py:16
  96.5 5.4 %all-to-all-start = ((bf16[32,256,768]{1,0,2:T(8,128)(2,1)}), bf16[32,256,768]{1,0,2:T(8,128)(2,1)}, u32[]{:S(2)}, u32[]{:S(2)}) async-start(bf16[32,256,768]{1,0,2:T(8,128)(2,1)} %divide_convert_fusion.1), calls=%async_computation | async-start | bytes 25165824 | tf_op jit(solution)/shard_map/all_to_all | solution.py:20
  101.9 25.1 %copy.25 = f32[32,256,768]{1,0,2:T(8,128)} copy(f32[32,256,768]{2,1,0:T(8,128)} %param.5) | data formatting | bytes 50331648 | tf_op args[1]
  127.2 14.1 %divide_convert_fusion = bf16[32,256,768]{1,0,2:T(8,128)(2,1)} fusion(f32[32,256,768]{1,0,2:T(8,128)} %copy.25, f32[32,768]{0,1:T(8,128)S(1)} %copy.24), kind=kLoop, calls=%fused_computation | loop fusion | flops 12582912 | bytes 37847040 | tf_op jit(solution)/shard_map/convert_element_type | solution.py:17
  141.3 99.6 %all-to-all-done = bf16[32,256,768]{1,0,2:T(8,128)(2,1)} async-done(((bf16[32,256,768]{1,0,2:T(8,128)(2,1)}), bf16[32,256,768]{1,0,2:T(8,128)(2,1)}, u32[]{:S(2)}, u32[]{:S(2)}) %all-to-all-start) | async-done | bytes 12582944 | tf_op jit(solution)/shard_map/all_to_all | solution.py:20
  240.9 5.3 %all-to-all-start.1 = ((bf16[32,256,768]{1,0,2:T(8,128)(2,1)}), bf16[32,256,768]{1,0,2:T(8,128)(2,1)}, u32[]{:S(2)}, u32[]{:S(2)}) async-start(bf16[32,256,768]{1,0,2:T(8,128)(2,1)} %divide_convert_fusion), calls=%async_computation.1 | async-start | bytes 25165824 | tf_op jit(solution)/shard_map/all_to_all | solution.py:21
  246.7 138.2 %collective-permute-done = bf16[256,32]{0,1:T(8,128)(2,1)S(1)} collective-permute-done((bf16[256,32]{0,1:T(8,128)(2,1)S(1)}, bf16[256,32]{0,1:T(8,128)(2,1)S(1)}, u32[]{:S(2)}, u32[]{:S(2)}) %collective-permute-start) | collective-permute-done | bytes 16416 | tf_op jit(solution)/shard_map/ppermute | solution.py:32
  384.9 4.1 collective-permute-done.1
  389.0 4.1 collective-permute-done.2
  393.0 4.1 collective-permute-done.3
  397.1 4.1 collective-permute-done.4
  401.1 4.1 collective-permute-done.5
  405.2 0.7 constant_dynamic-slice_fusion.2
  406.6 2.7 collective-permute-done.6
  409.5 16.2 %all_gather.3 = bf16[2048,128]{0,1:T(8,128)(2,1)S(1)} all-gather(bf16[2048,32]{0,1:T(8,128)(2,1)S(1)} %constant_dynamic-slice_fusion), channel_id=1, replica_groups=mesh['owner'=4,'rows'=8] {'owner'}, dimensions={1}, use_global_device_ids=true | all-gather | bytes 655360 | tf_op jit(solution)/shard_map/all_gather | solution.py:36
  425.6 1.0 copy.28
  426.6 14.1 %copy.23 = bf16[32,8,256,96]{2,1,3,0:T(8,128)(2,1)} copy(bf16[32,8,256,96]{2,0,3,1:T(8,128)(2,1)} %bitcast.2) | data formatting | bytes 25165824 | tf_op jit(solution)/shard_map/all_to_all | solution.py:20
  440.7 19.5 %all_to_all.29 = bf16[32,2048,96]{1,2,0:T(8,128)(2,1)} reshape(bf16[32,8,256,96]{2,1,3,0:T(8,128)(2,1)} %copy.23) | data formatting | bytes 25165824 | tf_op jit(solution)/shard_map/all_to_all | solution.py:20
  460.2 14.1 %copy.27 = bf16[32,8,256,96]{2,1,3,0:T(8,128)(2,1)} copy(bf16[32,8,256,96]{2,0,3,1:T(8,128)(2,1)} %bitcast.5) | data formatting | bytes 25165824 | tf_op jit(solution)/shard_map/all_to_all | solution.py:21
  474.2 19.5 %all_to_all.33 = bf16[32,2048,96]{1,2,0:T(8,128)(2,1)} reshape(bf16[32,8,256,96]{2,1,3,0:T(8,128)(2,1)} %copy.27) | data formatting | bytes 25165824 | tf_op jit(solution)/shard_map/all_to_all | solution.py:21
  (38 shorter events, 1.6 us)
Async XLA Ops:
  7.2 74.2 %all-reduce.3.cloned.1.call-start = ((), (), s32[]{:S(2)}) async-start(), calls=%async_computation.2 | async-start | bytes 393216 | tf_op jit(solution)/shard_map/psum | solution.py:10
  96.5 144.4 %all-to-all-start = ((bf16[32,256,768]{1,0,2:T(8,128)(2,1)}), bf16[32,256,768]{1,0,2:T(8,128)(2,1)}, u32[]{:S(2)}, u32[]{:S(2)}) async-start(bf16[32,256,768]{1,0,2:T(8,128)(2,1)} %divide_convert_fusion.1), calls=%async_computation | async-start | bytes 25165824 | tf_op jit(solution)/shard_map/all_to_all | solution.py:20
  101.9 25.1 %copy-start.1 = (f32[32,768]{1,0:T(8,128)S(1)}, f32[32,768]{1,0:T(8,128)}, u32[]{:S(2)}) copy-start(f32[32,768]{1,0:T(8,128)} %get-tuple-element.11) | copy-start | bytes 294916
  127.2 119.1 %copy-start = (f32[256,32]{0,1:T(8,128)S(1)}, f32[256,32]{0,1:T(8,128)}, u32[]{:S(2)}) copy-start(f32[256,32]{0,1:T(8,128)} %param.6) | copy-start | bytes 98308
  127.2 119.1 %copy-start.2 = (f32[256]{0:T(256)S(1)}, f32[256]{0:T(256)}, u32[]{:S(2)}) copy-start(f32[256]{0:T(256)} %param.7) | copy-start | bytes 3076
  240.9 219.3 %all-to-all-start.1 = ((bf16[32,256,768]{1,0,2:T(8,128)(2,1)}), bf16[32,256,768]{1,0,2:T(8,128)(2,1)}, u32[]{:S(2)}, u32[]{:S(2)}) async-start(bf16[32,256,768]{1,0,2:T(8,128)(2,1)} %divide_convert_fusion), calls=%async_computation.1 | async-start | bytes 25165824 | tf_op jit(solution)/shard_map/all_to_all | solution.py:21
  246.3 138.6 %collective-permute-start = (bf16[256,32]{0,1:T(8,128)(2,1)S(1)}, bf16[256,32]{0,1:T(8,128)(2,1)S(1)}, u32[]{:S(2)}, u32[]{:S(2)}) collective-permute-start(bf16[256,32]{0,1:T(8,128)(2,1)S(1)} %multiply_convert_fusion), channel_id=1, source_target_pairs={{0,1},{1,2},{2,3},{3,4},{4,5},{5,6},{6,7},{7,0},{8,9},{9,10},{10,1... | collective-permute-start | bytes 49160 | tf_op jit(solution)/shard_map/ppermute | solution.py:32
  384.9 4.1 collective-permute-start.1
  388.9 4.1 collective-permute-start.2
  393.0 4.1 collective-permute-start.3
  397.1 4.1 collective-permute-start.4
  401.1 4.1 collective-permute-start.5
  405.2 4.1 collective-permute-start.6
Sparse Core Ops, SparseCore 0:
  24.8 56.4 all-reduce.2
